TPU v7x, 32 devices: a whole 2x2x4 slice. The times are simulated.
32 devices in a mesh: seq: 8 (over y, x, core), head: 4 (over z).
Axes of the slice: x: 2, y: 2, z: 4, core: 2. Of those that a mesh axis runs over, the one named last changes fastest.
Arguments:
- queries: bfloat16 [2048, 1024], P('seq', 'head'), may hold values from -6 to 6
- keys: bfloat16 [2048, 1024], P('seq', 'head'), may hold values from -6 to 6
- values: bfloat16 [2048, 1024], P('seq', 'head'), may hold values from -6 to 6
- gate: bfloat16 [2048, 1024], P('seq', 'head'), may hold values from -6 to 6
- log_forget: float32 [8, 2048], P('head', 'seq'), may hold values from -1.5 to 0
- write_rate: float32 [8, 2048], P('head', 'seq'), may hold values from 0 to 1
- level_weight: float32 [8, 6, 2048], P('head', None, 'seq'), may hold values from 0.25 to 2.5
- w_out: bfloat16 [1024, 4096], P('head'), may hold values from -0.1875 to 0.1875
Outputs:
- mixed: bfloat16 [2048, 4096], P(('seq', 'head'))
All inputs are finite; a program needn't handle non-finite values.
Results may differ from a plain program's by a relative error of at most 0.02.
Values may be sent and summed in bfloat16 or wider, within the bound.
A program may use at most 64 MiB of HBM per device.

v0:
```python
import jax
import jax.numpy as jnp
from jax import lax
from jax.sharding import PartitionSpec as P

DK = 128
BLOCK = 64


EPSILON = 1e-06
PRECISE = lax.Precision.HIGHEST


def as_sent(shard):

    def short(part):
        return part.astype(jnp.bfloat16) if part.dtype == jnp.float32 else part

    return jax.tree.map(short, shard)


def swapped(block, axis, stride):
    count = lax.axis_size(axis)
    route = []
    for low in range(count):
        high = low | 1 << stride
        if high != low and high < count:
            route += [(low, high), (high, low)]
    return lax.ppermute(block, axis, route)


def unit_rows(matrix):
    floated = matrix.astype(jnp.float32)
    return floated * lax.rsqrt(jnp.sum(floated * floated, axis=-1, keepdims=True) + EPSILON)


def matmul(left, right):
    return jnp.einsum("...ij,...jk->...ik", left, right, precision=PRECISE)


def compose(leading, trailing):
    return (matmul(leading[0], trailing[1]) + trailing[0], matmul(leading[1], trailing[1]))


def partner_blocks(tensor, stride):
    shaped = tensor.reshape(
        tensor.shape[0],
        tensor.shape[1] // (2 * stride),
        2,
        stride,
        tensor.shape[2],
        tensor.shape[3],
    )
    return jnp.flip(shaped, axis=2).reshape(tensor.shape)


def on_device(queries, keys, values, gate, log_forget, write_rate, level_weight, w_out):
    tokens_here = queries.shape[0]
    heads_here = log_forget.shape[0]
    blocks = tokens_here // BLOCK
    inner_bits = blocks.bit_length() - 1
    outer_bits = lax.axis_size("seq").bit_length() - 1

    def arrange(matrix):
        return jnp.transpose(matrix.reshape(blocks, BLOCK, heads_here, DK), (2, 0, 1, 3))

    query_rows = arrange(unit_rows(queries.reshape(tokens_here, heads_here, DK)))
    key_rows = arrange(unit_rows(keys.reshape(tokens_here, heads_here, DK)))
    value_rows = arrange(values.astype(jnp.float32))
    decay_logs = log_forget.reshape(heads_here, blocks, BLOCK)
    strength = write_rate.reshape(heads_here, blocks, BLOCK)
    rows_index = lax.broadcasted_iota(jnp.int32, (BLOCK, BLOCK), 0)
    cols_index = lax.broadcasted_iota(jnp.int32, (BLOCK, BLOCK), 1)
    inclusive = rows_index >= cols_index
    strict = rows_index > cols_index
    cumulative = jnp.einsum(
        "hnc,tc->hnt", decay_logs, inclusive.astype(jnp.float32), precision=PRECISE
    )
    spread = cumulative[..., :, None] - cumulative[..., None, :]
    fading = jnp.exp(jnp.where(inclusive, spread, -1e30))
    key_key = jnp.einsum("hncd,hnsd->hncs", key_rows, key_rows, precision=PRECISE)
    query_key = jnp.einsum("hncd,hnsd->hncs", query_rows, key_rows, precision=PRECISE)
    unit_block = jnp.eye(BLOCK, dtype=jnp.float32)
    rated_keys = strength[..., :, None] * key_key
    lower_keys = unit_block + jnp.where(strict, rated_keys, 0.0)
    lower_values = unit_block + jnp.where(strict, rated_keys * fading, 0.0)
    key_bases = jax.scipy.linalg.solve_triangular(
        lower_keys, strength[..., None] * key_rows, lower=True, unit_diagonal=True
    )
    writes = jax.scipy.linalg.solve_triangular(
        lower_values, strength[..., None] * value_rows, lower=True, unit_diagonal=True
    )
    reach_rows = jnp.exp(cumulative)[..., None] * (
        query_rows
        - jnp.einsum(
            "hnts,hnsd->hntd", jnp.where(inclusive, query_key, 0.0), key_bases, precision=PRECISE
        )
    )
    own_read = jnp.einsum("hnts,hnsd->hntd", query_key * fading, writes, precision=PRECISE)
    final_log = cumulative[..., -1]
    unit_state = jnp.eye(DK, dtype=jnp.float32)
    moving = jnp.exp(final_log)[..., None, None] * (
        unit_state - jnp.einsum("hnti,hntj->hnij", key_bases, key_rows, precision=PRECISE)
    )
    tail_decay = jnp.exp(final_log[..., None] - cumulative)
    ending = jnp.einsum(
        "hnti,hntj->hnij", writes * tail_decay[..., None], key_rows, precision=PRECISE
    )
    totals = (ending, moving)
    prefix = jnp.broadcast_to(unit_state, (heads_here, blocks, DK, DK))
    inner_levels = []
    block_ids = jnp.arange(blocks, dtype=jnp.int32)
    for exponent in range(inner_bits):
        stride = 2**exponent
        partner = (partner_blocks(totals[0], stride), partner_blocks(totals[1], stride))
        upper_half = (block_ids // stride % 2 == 1)[None, :, None, None]
        inner_levels.append(jnp.where(upper_half, matmul(partner[0], prefix), 0.0))
        prefix = jnp.where(upper_half, matmul(partner[1], prefix), prefix)
        leading = (
            jnp.where(upper_half, partner[0], totals[0]),
            jnp.where(upper_half, partner[1], totals[1]),
        )
        trailing = (
            jnp.where(upper_half, totals[0], partner[0]),
            jnp.where(upper_half, totals[1], partner[1]),
        )
        totals = compose(leading, trailing)
    slab_end = totals[0][:, 0]
    slab_move = totals[1][:, 0]
    position = lax.axis_index("seq")
    identity_heads = jnp.broadcast_to(unit_state, (heads_here, DK, DK))
    totals_here = (slab_end, slab_move)
    before = identity_heads
    collected = []
    for exponent in range(outer_bits):
        partner = swapped((as_sent(totals_here[0]), as_sent(totals_here[1])), "seq", exponent)
        upper_half = position // 2**exponent % 2 == 1
        collected.append(jnp.where(upper_half, matmul(partner[0], before), 0.0))
        before = jnp.where(upper_half, matmul(partner[1], before), before)
        leading = (
            jnp.where(upper_half, partner[0], totals_here[0]),
            jnp.where(upper_half, partner[1], totals_here[1]),
        )
        trailing = (
            jnp.where(upper_half, totals_here[0], partner[0]),
            jnp.where(upper_half, totals_here[1], partner[1]),
        )
        totals_here = compose(leading, trailing)
    outer_levels = jnp.stack(collected)
    weights = level_weight.reshape(heads_here, level_weight.shape[1], blocks, BLOCK)
    core_rows = weights[:, 0, :, :, None] * own_read
    stacked = jnp.stack(inner_levels, axis=1)
    level_reads = jnp.einsum("hlnij,hncj->hlnci", stacked, reach_rows, precision=PRECISE)
    core_rows = core_rows + jnp.einsum(
        "hlnc,hlnci->hnci", weights[:, 1 : 1 + inner_bits], level_reads, precision=PRECISE
    )
    lifted = jnp.einsum("hnij,hncj->hnci", prefix, reach_rows, precision=PRECISE)
    cross_reads = jnp.einsum("lhij,hncj->hlnci", outer_levels, lifted, precision=PRECISE)
    core_rows = core_rows + jnp.einsum(
        "hlnc,hlnci->hnci", weights[:, 1 + inner_bits :], cross_reads, precision=PRECISE
    )
    core_rows = jnp.transpose(core_rows, (1, 2, 0, 3)).reshape(tokens_here, heads_here, DK)
    scaled = core_rows * lax.rsqrt(
        jnp.mean(core_rows * core_rows, axis=-1, keepdims=True) + EPSILON
    )
    gated = scaled * jax.nn.silu(gate.astype(jnp.float32).reshape(tokens_here, heads_here, DK))
    normed = gated.reshape(tokens_here, heads_here * DK).astype(jnp.bfloat16)
    return lax.psum_scatter(
        jnp.dot(normed, w_out, preferred_element_type=jnp.float32).astype(jnp.bfloat16),
        "head",
        scatter_dimension=0,
        tiled=True,
    )


def solution(mesh):
    in_specs = (
        P("seq", "head"),
        P("seq", "head"),
        P("seq", "head"),
        P("seq", "head"),
        P("head", "seq"),
        P("head", "seq"),
        P("head", None, "seq"),
        P("head", None),
    )
    out_specs = P(("seq", "head"), None)
    return jax.shard_map(
        on_device, mesh=mesh, in_specs=in_specs, out_specs=out_specs, check_vma=False
    )
```

profile of v0, /device:TPU:0, one launch (start us, length us, event | category | flops | bytes accessed | tf_op | source)
XLA Modules:
  0.0 214.4 jit_solution(1068323615153228488)
XLA Ops:
  13.5 1.4 add_bitcast_fusion.1
  14.9 39.3 %custom-call.4 = f32[2,4,1,64,64]{3,4,2,1,0:T(8,128)S(1)} custom-call(f32[2,4,1,64,64]{4,3,2,1,0:T(8,128)S(1)} %get-tuple-element.10), custom_call_target="InvertDiagBlocksLowerTriangular" | custom-call | tf_op jit(solution)/shard_map/jit(_solve_triangular)/vmap(vmap())/triangular_solve | solution.py:90
  54.2 40.2 %custom-call.5 = f32[2,4,1,64,64]{3,4,2,1,0:T(8,128)S(1)} custom-call(f32[2,4,1,64,64]{4,3,2,1,0:T(8,128)} %get-tuple-element.11), custom_call_target="InvertDiagBlocksLowerTriangular" | custom-call | tf_op jit(solution)/shard_map/jit(_solve_triangular)/vmap(vmap())/triangular_solve | solution.py:87
  94.5 1.5 fusion.29
  98.7 2.0 fusion.2
  100.9 1.5 fusion.18
  102.4 1.6 convolution_add_fusion
  105.1 1.9 rev.17
  116.6 1.7 reshape.176
  118.3 1.7 convert_multiply_fusion.2
  120.0 2.4 %fusion = f32[2,1,4,128,128]{4,3,2,0,1:T(8,128)} fusion(f32[2,4,128,128]{3,2,1,0:T(8,128)} %bitcast.156, f32[128,128]{1,0:T(8,128)S(1)} %fusion.73, pred[4]{0:T(512)(128)(4,1)} %copy-done.18), kind=kOutput, calls=%fused_computation.6 | convolution fusion | flops 201457664 | bytes 1114116 | tf_op jit(solution)/shard_map/...ij,...jk->...ik/dot_general | solution.py:38
  123.7 1.5 fusion.1
  125.1 1.4 convolution_select_fusion
  126.6 1.6 copy.40
  131.5 2.5 %convolution_bitcast_fusion.1 = f32[2,2,4,64,128]{4,3,1,2,0:T(8,128)S(1)} fusion(f32[2,4,64,128]{3,2,1,0:T(8,128)S(1)} %fusion.3, f32[2,1,4,128,128]{4,3,2,0,1:T(8,128)} %fusion.1, f32[2,1,4,128,128]{4,3,2,0,1:T(8,128)} %fusion), kind=kOutput, calls=%fused_computation.8 | convolution fusion | flops 201588736 | bytes 1835008 | tf_op jit(solution)/shard_map/hlnij,hncj->hlnci/dot_general | solution.py:153
  134.0 4.7 %fusion.21 = f32[2,4,64,1,128]{4,3,2,1,0:T(1,128)} fusion(f32[2,2,4,64,1]{1,4,3,2,0:T(1,128)S(1)} %copy-done.14, f32[2,2,4,64,128]{4,3,1,2,0:T(8,128)S(1)} %convolution_bitcast_fusion.1), kind=kOutput, calls=%fused_computation.44 | convolution fusion | flops 1572864 | bytes 790528 | tf_op jit(solution)/shard_map/hlnc,hlnci->hnci/dot_general | solution.py:154
  139.9 1.6 copy.48
  141.8 3.0 %collective-permute-start.3 = (bf16[2,128,128]{2,1,0:T(8,128)(2,1)S(1)}, bf16[2,128,128]{2,1,0:T(8,128)(2,1)S(1)}, u32[]{:S(2)}, u32[]{:S(2)}) collective-permute-start(bf16[2,128,128]{2,1,0:T(8,128)(2,1)S(1)} %get-tuple-element.18), channel_id=1, source_target_pairs={{0,8},{8,0},{4,12},{12,4},{16,24},{24,16},{20,28},{28,20},{1,9},{9... | collective-permute-start | bytes 196616 | tf_op jit(solution)/shard_map/ppermute | solution.py:29
  147.4 3.0 %collective-permute-done.2 = bf16[2,128,128]{2,1,0:T(8,128)(2,1)S(1)} collective-permute-done((bf16[2,128,128]{2,1,0:T(8,128)(2,1)S(1)}, bf16[2,128,128]{2,1,0:T(8,128)(2,1)S(1)}, u32[]{:S(2)}, u32[]{:S(2)}) %collective-permute-start.2) | collective-permute-done | bytes 65568 | tf_op jit(solution)/shard_map/ppermute | solution.py:29
  150.7 1.6 collective-permute-start.4
  152.7 2.3 %collective-permute-done.4 = bf16[2,128,128]{2,1,0:T(8,128)(2,1)S(1)} collective-permute-done((bf16[2,128,128]{2,1,0:T(8,128)(2,1)S(1)}, bf16[2,128,128]{2,1,0:T(8,128)(2,1)S(1)}, u32[]{:S(2)}, u32[]{:S(2)}) %collective-permute-start.4) | collective-permute-done | bytes 65568 | tf_op jit(solution)/shard_map/ppermute | solution.py:29
  156.0 3.9 %fusion.12 = f32[2,4,64,1,128]{4,3,2,1,0:T(1,128)S(1)} fusion(f32[2,3,4,64,1]{1,4,3,2,0:T(1,128)S(1)} %copy-done.13, f32[2,3,4,64,128]{4,3,1,2,0:T(8,128)S(1)} %convolution_bitcast_fusion), kind=kOutput, calls=%fused_computation.35 | convolution fusion | flops 2359296 | bytes 1054720 | tf_op jit(solution)/shard_map/hlnc,hlnci->hnci/dot_general | solution.py:159
  161.3 2.1 convolution_convert_fusion
  163.4 44.1 %reduce-scatter.2.cloned.1.call-done = bf16[64,4096]{1,0:T(8,128)(2,1)} async-done(((bf16[256,4096]{1,0:T(8,128)(2,1)}), bf16[64,4096]{1,0:T(8,128)(2,1)}) %reduce-scatter.2.cloned.1.call-update) | async-done | bytes 524304 | tf_op jit(solution)/shard_map/reduce_scatter | solution.py:168
  (109 shorter events, 31.9 us)
Async XLA Ops:
  6.5 154.7 %copy-start = (bf16[256,4096]{1,0:T(8,128)(2,1)S(1)}, bf16[256,4096]{1,0:T(8,128)(2,1)}, u32[]{:S(2)}) copy-start(bf16[256,4096]{1,0:T(8,128)(2,1)} %param.17) | copy-start | bytes 6291460
  6.5 201.0 %reduce-scatter.2.cloned.1.call-start = ((), (), s32[]{:S(2)}) async-start(), calls=%async_computation.1 | async-start | bytes 2621440 | tf_op jit(solution)/shard_map/reduce_scatter | solution.py:168
  6.5 102.5 %copy-start.20 = (pred[4]{0:T(512)(128)(4,1)}, pred[4]{0:T(512)(128)(4,1)S(1)}, u32[]{:S(2)}) copy-start(pred[4]{0:T(512)(128)(4,1)S(1)} %fusion.81) | copy-start | bytes 16
  6.6 95.8 %copy-start.18 = (pred[4]{0:T(512)(128)(4,1)}, pred[4]{0:T(512)(128)(4,1)S(1)}, u32[]{:S(2)}) copy-start(pred[4]{0:T(512)(128)(4,1)S(1)} %fusion.80) | copy-start | bytes 16
  14.9 83.8 %copy-start.22 = (f32[2,4]{1,0:T(2,128)S(1)}, f32[2,4]{1,0:T(2,128)}, u32[]{:S(2)}) copy-start(f32[2,4]{1,0:T(2,128)} %exp.24) | copy-start | bytes 100
  97.8 3.0 %copy-start.4 = (f32[2,4,128,128]{3,2,1,0:T(8,128)}, f32[2,4,128,128]{3,2,1,0:T(8,128)S(1)}, u32[]{:S(2)}) copy-start(f32[2,4,128,128]{3,2,1,0:T(8,128)S(1)} %fusion.34) | copy-start | bytes 1572868
  109.8 35.0 %collective-permute-start = (bf16[2,128,128]{2,1,0:T(8,128)(2,1)}, bf16[2,128,128]{2,1,0:T(8,128)(2,1)}, u32[]{:S(2)}, u32[]{:S(2)}) collective-permute-start(bf16[2,128,128]{2,1,0:T(8,128)(2,1)} %get-tuple-element.6), channel_id=1, source_target_pairs={{0,4},{4,0},{8,12},{12,8},{16,20},{20,16},{24,28},{28,24},{1,5},{5... | collective-permute-start | bytes 196616 | tf_op jit(solution)/shard_map/ppermute | solution.py:29
  111.3 30.2 %collective-permute-start.1 = (bf16[2,128,128]{2,1,0:T(8,128)(2,1)}, bf16[2,128,128]{2,1,0:T(8,128)(2,1)S(1)}, u32[]{:S(2)}, u32[]{:S(2)}) collective-permute-start(bf16[2,128,128]{2,1,0:T(8,128)(2,1)} %get-tuple-element.14), channel_id=1, source_target_pairs={{0,4},{4,0},{8,12},{12,8},{16,20},{20,16},{24,28},{28,24},{1,5},{5... | collective-permute-start | bytes 196616 | tf_op jit(solution)/shard_map/ppermute | solution.py:29
  118.3 5.3 %copy-start.21 = (pred[4]{0:T(512)(128)(4,1)S(1)}, pred[4]{0:T(512)(128)(4,1)}, u32[]{:S(2)}) copy-start(pred[4]{0:T(512)(128)(4,1)} %copy-done.20) | copy-start | bytes 16
  118.3 6.8 %copy-start.3 = (f32[2,1,2,2,128,128]{5,4,3,2,0,1:T(8,128)S(1)}, f32[2,1,2,2,128,128]{5,4,3,2,0,1:T(8,128)}, u32[]{:S(2)}) copy-start(f32[2,1,2,2,128,128]{5,4,3,2,0,1:T(8,128)} %rev.17) | copy-start | bytes 1572868
  123.7 6.0 %copy-start.7 = (f32[4,64,2,128]{3,2,1,0:T(2,128)S(1)}, f32[4,64,2,128]{3,2,1,0:T(2,128)}, u32[]{:S(2)}) copy-start(f32[4,64,2,128]{3,2,1,0:T(2,128)} %reshape.176) | copy-start | bytes 786436
  125.1 5.3 %copy-start.6 = (f32[2,4,64,128]{3,2,1,0:T(8,128)S(1)}, f32[2,4,64,128]{3,2,1,0:T(8,128)}, u32[]{:S(2)}) copy-start(f32[2,4,64,128]{3,2,1,0:T(8,128)} %fusion.29) | copy-start | bytes 786436
  129.7 4.3 %copy-start.14 = (f32[2,2,4,64,1]{1,4,3,2,0:T(1,128)S(1)}, f32[2,2,4,64,1]{1,4,3,2,0:T(1,128)}, u32[]{:S(2)}) copy-start(f32[2,2,4,64,1]{1,4,3,2,0:T(1,128)} %copy.40) | copy-start | bytes 12292
  131.5 7.2 %copy-start.10 = (f32[2,4,128,128]{3,2,1,0:T(8,128)S(1)}, f32[2,4,128,128]{3,2,1,0:T(8,128)}, u32[]{:S(2)}) copy-start(f32[2,4,128,128]{3,2,1,0:T(8,128)} %convolution_select_fusion) | copy-start | bytes 1572868
  134.0 7.5 %copy-start.11 = (f32[2,128,128]{2,1,0:T(8,128)S(1)}, f32[2,128,128]{2,1,0:T(8,128)}, u32[]{:S(2)}) copy-start(f32[2,128,128]{2,1,0:T(8,128)} %get-tuple-element.15) | copy-start | bytes 393220
  134.0 10.8 %copy-start.12 = (f32[2,128,128]{2,1,0:T(8,128)S(1)}, f32[2,128,128]{2,1,0:T(8,128)}, u32[]{:S(2)}) copy-start(f32[2,128,128]{2,1,0:T(8,128)} %get-tuple-element.7) | copy-start | bytes 393220
  141.8 14.2 %copy-start.13 = (f32[2,3,4,64,1]{1,4,3,2,0:T(1,128)S(1)}, f32[2,3,4,64,1]{1,4,3,2,0:T(1,128)}, u32[]{:S(2)}) copy-start(f32[2,3,4,64,1]{1,4,3,2,0:T(1,128)} %copy.48) | copy-start | bytes 18436
  141.8 5.6 %collective-permute-start.3 = (bf16[2,128,128]{2,1,0:T(8,128)(2,1)S(1)}, bf16[2,128,128]{2,1,0:T(8,128)(2,1)S(1)}, u32[]{:S(2)}, u32[]{:S(2)}) collective-permute-start(bf16[2,128,128]{2,1,0:T(8,128)(2,1)S(1)} %get-tuple-element.18), channel_id=1, source_target_pairs={{0,8},{8,0},{4,12},{12,4},{16,24},{24,16},{20,28},{28,20},{1,9},{9... | collective-permute-start | bytes 196616 | tf_op jit(solution)/shard_map/ppermute | solution.py:29
  146.0 4.3 %collective-permute-start.2 = (bf16[2,128,128]{2,1,0:T(8,128)(2,1)S(1)}, bf16[2,128,128]{2,1,0:T(8,128)(2,1)S(1)}, u32[]{:S(2)}, u32[]{:S(2)}) collective-permute-start(bf16[2,128,128]{2,1,0:T(8,128)(2,1)S(1)} %get-tuple-element.16), channel_id=1, source_target_pairs={{0,8},{8,0},{4,12},{12,4},{16,24},{24,16},{20,28},{28,20},{1,9},{9... | collective-permute-start | bytes 196616 | tf_op jit(solution)/shard_map/ppermute | solution.py:29
  150.7 4.3 %collective-permute-start.4 = (bf16[2,128,128]{2,1,0:T(8,128)(2,1)S(1)}, bf16[2,128,128]{2,1,0:T(8,128)(2,1)S(1)}, u32[]{:S(2)}, u32[]{:S(2)}) collective-permute-start(bf16[2,128,128]{2,1,0:T(8,128)(2,1)S(1)} %fusion.10), channel_id=1, source_target_pairs={{0,16},{16,0},{4,20},{20,4},{8,24},{24,8},{12,28},{28,12},{1,17},{... | collective-permute-start | bytes 196616 | tf_op jit(solution)/shard_map/ppermute | solution.py:29
  152.5 7.5 %copy-start.9 = (f32[2,4,64,128]{3,2,1,0:T(8,128)S(1)}, f32[2,4,64,128]{3,2,1,0:T(8,128)}, u32[]{:S(2)}) copy-start(f32[2,4,64,128]{3,2,1,0:T(8,128)} %copy-done.8) | copy-start | bytes 786436
  152.5 7.5 %copy-start.15 = (f32[2,4,64,1,128]{4,3,2,1,0:T(1,128)S(1)}, f32[2,4,64,1,128]{4,3,2,1,0:T(1,128)}, u32[]{:S(2)}) copy-start(f32[2,4,64,1,128]{4,3,2,1,0:T(1,128)} %fusion.21) | copy-start | bytes 786436
  152.5 7.5 %copy-start.19 = (f32[4,64,2]{1,0,2:T(4,128)S(1)}, f32[4,64,2]{1,0,2:T(4,128)}, u32[]{:S(2)}) copy-start(f32[4,64,2]{1,0,2:T(4,128)} %slice_bitcast_fusion.2) | copy-start | bytes 6148
  156.0 5.3 %copy-start.16 = (bf16[256,256]{1,0:T(8,128)(2,1)S(1)}, bf16[256,256]{1,0:T(8,128)(2,1)}, u32[]{:S(2)}) copy-start(bf16[256,256]{1,0:T(8,128)(2,1)} %param.13) | copy-start | bytes 393220
  (5 other events, 6.4 us)
Sparse Core Ops, SparseCore 0:
  163.5 43.9 reduce-scatter.1
where the time goes:
time: 215 us; the launch traced here: 214 us
  other arithmetic  85.8 us (40%)
  waiting for transfers between devices  49.4 us (23%)
  matrix products  39.3 us (18%)
  local copies, waits for them, and re-layouts  20.7 us (10%)
  between operations  14 us (7%)
  starting transfers between devices  5.23 us (2%)
    reduce_scatter x1, waiting for transfers between devices, on_device(): lax.psum_scatter(jnp.dot(normed, w_out, preferred_element_type=jnp.float3...  44.1 us
    another operation x1, other arithmetic, on_device(): jax.scipy.linalg.solve_triangular(lower_keys, strength[..., None] * key_r...  40.2 us
    another operation x4, other arithmetic, on_device(): jax.scipy.linalg.solve_triangular(lower_values, strength[..., None] * val...  39.4 us
    dot_general x15, matrix products, matmul(): return jnp.einsum('...ij,...jk->...ik', left, right, precision=PRECISE)  14 us
    ppermute x5, waiting for transfers between devices, swapped(): return lax.ppermute(block, axis, route)  5.25 us
    ppermute x5, starting transfers between devices, swapped(): return lax.ppermute(block, axis, route)  5.23 us
    dot_general x1, matrix products, on_device(): jnp.einsum('hlnc,hlnci->hnci', weights[:, 1:1 + inner_bits], level_reads,...  4.68 us
  transfers between devices with their start and end apart: 6, of which 3 were waited for; matrix products, arithmetic and copies ran while one was open for 16% of the time, Pallas kernels for 0%

commit v1 on v0

v1 whole, which is shorter than its diff:
```python
import functools

import jax
import jax.numpy as jnp
from jax import lax
from jax.experimental import pallas as pl
from jax.experimental.pallas import tpu as pltpu
from jax.sharding import PartitionSpec as P

DK = 128
BLOCK = 64
EPSILON = 1e-06
F32 = jnp.float32
BF16 = jnp.bfloat16
MESH = pl.DeviceIdType.MESH


def dot(left, right):
    return jnp.dot(left.astype(BF16), right.astype(BF16), preferred_element_type=F32)


def dot_nt(left, right):
    return lax.dot_general(
        left.astype(BF16), right.astype(BF16), (((1,), (1,)), ((), ())), preferred_element_type=F32
    )


def unit_rows(ref, cols):
    floated = ref[:, cols].astype(F32)
    return floated * lax.rsqrt(jnp.sum(floated * floated, axis=-1, keepdims=True) + EPSILON)


def kernel(
    ns, nz, heads, levels,
    q_ref, k_ref, v_ref, g_ref, lf_ref, wr_ref, lw_ref, w_ref, o_ref,
    stage, wbuf, ebuf, pbuf, tbuf, sbuf, hbuf, pm, mbuf, nbuf, gbuf, ybuf, obuf,
    wl_sem, ws_sem, wr_sem, ds_sem, dr_sem, ps_sem, pr_sem, ss_sem, sr_sem,
    ns_sem, nr_sem, gs_sem, gr_sem, os_sem, or_sem,
):
    tok = q_ref.shape[0]
    nq = ns // 2
    width = wbuf.shape[2]
    half = width // 2
    rows = tok // nz
    inner_bits = (tok // BLOCK).bit_length() - 1
    chip_bits = nq.bit_length() - 1
    s = lax.axis_index("seq")
    z = lax.axis_index("head")
    q = s // 2
    c = lax.rem(s, 2)
    partner = s + 1 - 2 * c

    def to(seq, head):
        return {"device_id": (seq, head), "device_id_type": MESH}

    def zpeer(d):
        return lax.rem(z + d, nz)

    def zfrom(d):
        return lax.rem(z + nz - d, nz)

    def qpeer(d):
        return 2 * lax.rem(q + d, nq) + c

    def qfrom(d):
        return lax.rem(q + nq - d, nq)

    barrier = pltpu.get_barrier_semaphore()
    for d in range(1, nz):
        pl.semaphore_signal(barrier, inc=1, **to(s, zpeer(d)))
    pl.semaphore_signal(barrier, inc=1, **to(partner, z))
    for d in range(1, nq):
        pl.semaphore_signal(barrier, inc=1, **to(qpeer(d), z))

    chip_cols = pl.ds(pl.multiple_of(q * width, width), width)
    mine = pl.ds(pl.multiple_of(s * half, half), half)
    my_half = pl.ds(pl.multiple_of(c * half, half), half)
    local_w = pltpu.make_async_copy(w_ref.at[:, chip_cols], wbuf.at[z], wl_sem)
    local_w.start()
    pl.semaphore_wait(barrier, nz + nq - 1)

    w_copies = [
        pltpu.make_async_remote_copy(
            w_ref.at[:, mine], wbuf.at[z, :, my_half], ws_sem.at[d - 1], wr_sem.at[d - 1],
            **to(s, zpeer(d)),
        )
        for d in range(1, nz)
    ]
    for copy in w_copies:
        copy.start()

    stage[...] = jnp.zeros_like(stage)
    stage[0:heads, :] = lf_ref[...]
    ti = lax.broadcasted_iota(jnp.int32, (tok, tok), 0)
    ui = lax.broadcasted_iota(jnp.int32, (tok, tok), 1)
    upto = jnp.where(ti <= ui, 1.0, 0.0).astype(F32)
    stage[0:8, :] = jnp.dot(
        stage[0:8, :], upto, precision=lax.Precision.HIGHEST, preferred_element_type=F32
    )
    stage[8 : 8 + heads, :] = wr_ref[...]
    for h in range(heads):
        stage[16 + h * levels : 16 + (h + 1) * levels, :] = lw_ref[h]
    cols = stage[...].T
    differ = lax.bitwise_xor(ti, ui)
    inclusive = ti >= ui

    hs = range(heads)
    span = [slice(h * DK, (h + 1) * DK) for h in hs]
    c_col = [cols[:, h : h + 1] for h in hs]
    b_col = [cols[:, 8 + h : 9 + h] for h in hs]

    def weight(h, level):
        at = 16 + h * levels + level
        return cols[:, at : at + 1]

    kn = [unit_rows(k_ref, span[h]) for h in hs]
    qn = [unit_rows(q_ref, span[h]) for h in hs]
    kb = [kn[h].astype(BF16) for h in hs]
    low = [jnp.where(ti > ui, b_col[h] * dot_nt(kb[h], kb[h]), 0.0) for h in hs]
    eye = jnp.where(ti == ui, 1.0, 0.0).astype(F32)
    inv = [eye - jnp.where(differ == 1, low[h], 0.0) for h in hs]
    bit = 1
    while 2**bit < tok:
        part = [jnp.where(differ >> bit == 1, low[h], 0.0) for h in hs]
        step = [dot(part[h], inv[h]) for h in hs]
        inv = [inv[h] - dot(inv[h], step[h]) for h in hs]
        bit += 1
    for h in hs:
        low_hi = low[h].astype(BF16)
        low_lo = (low[h] - low_hi.astype(F32)).astype(BF16)
        inv_hi = inv[h].astype(BF16)
        inv_lo = (inv[h] - inv_hi.astype(F32)).astype(BF16)
        residual = eye - inv[h] - (dot(low_hi, inv_hi) + (dot(low_hi, inv_lo) + dot(low_lo, inv_hi)))
        inv[h] = inv[h] + dot(inv_hi, residual)
    fade = [
        jnp.exp(jnp.where(inclusive, c_col[h] - stage[h : h + 1, :], -1e30)) for h in hs
    ]
    bk = [b_col[h] * kn[h] for h in hs]
    bv = [b_col[h] * v_ref[:, span[h]].astype(F32) for h in hs]
    eye_k = jnp.where(
        lax.broadcasted_iota(jnp.int32, (DK, DK), 0) == lax.broadcasted_iota(jnp.int32, (DK, DK), 1),
        1.0, 0.0,
    ).astype(F32)
    for h in hs:
        last = stage[h : h + 1, tok - 1 : tok]
        bases = dot(inv[h], bk[h])
        writes = dot(inv[h] * fade[h], bv[h])
        tail = jnp.exp(last - c_col[h])
        ebuf[h, 0] = dot((writes * tail).T, kb[h]).astype(BF16)
        ebuf[h, 1] = (jnp.exp(last) * (eye_k - dot(bases.T, kb[h]))).astype(BF16)
    pair = pltpu.make_async_remote_copy(ebuf, pbuf, ps_sem, pr_sem, **to(partner, z))
    pair.start()
    reads = [dot(jnp.where(inclusive, dot_nt(qn[h], kb[h]), 0.0), inv[h]) for h in hs]
    lifted = [jnp.exp(c_col[h]) * (qn[h] - dot(reads[h], bk[h])) for h in hs]
    core = []
    for h in hs:
        spread = weight(h, inner_bits)
        for level in reversed(range(inner_bits)):
            spread = jnp.where(differ < BLOCK * 2**level, weight(h, level), spread)
        core.append(dot(reads[h] * fade[h] * spread, bv[h]))

    pair.wait_recv()
    odd = c == 1
    for h in hs:
        e_own, m_own = ebuf[h, 0].astype(F32), ebuf[h, 1].astype(F32)
        e_oth, m_oth = pbuf[h, 0].astype(F32), pbuf[h, 1].astype(F32)
        e_a, e_b = jnp.where(odd, e_oth, e_own), jnp.where(odd, e_own, e_oth)
        m_a, m_b = jnp.where(odd, m_oth, m_own), jnp.where(odd, m_own, m_oth)
        tbuf[h, 0] = (dot(e_a, m_b) + e_b).astype(BF16)
        tbuf[h, 1] = dot(m_a, m_b).astype(BF16)
        hbuf[h, 0] = jnp.where(odd, e_oth, 0.0)
        for level in range(1, chip_bits + 1):
            hbuf[h, level] = jnp.zeros((DK, DK), F32)
        pm[h] = jnp.where(odd, m_oth, eye_k)

    def state_copy(d):
        return pltpu.make_async_remote_copy(
            tbuf, sbuf.at[d - 1], ss_sem.at[d - 1], sr_sem.at[d - 1], **to(qpeer(d), z)
        )

    for d in range(1, nq):
        @pl.when(q + d < nq)
        def _():
            state_copy(d).start()

    gates = []
    for h in hs:
        u = g_ref[:, span[h]].astype(F32)
        gates.append(u / (1.0 + jnp.exp(-u)))

    for d in range(1, nq):
        @pl.when(q >= d)
        def _():
            state_copy(d).wait_recv()
            source = q - d
            level = 0
            for k in range(chip_bits):
                level = level + (source // 2**k != q // 2**k).astype(jnp.int32)
            for h in hs:
                chain = pm[h].astype(BF16)
                hbuf[h, level] += dot(sbuf[d - 1, h, 0], chain)
                pm[h] = dot(sbuf[d - 1, h, 1], chain)

    for h in hs:
        total = core[h]
        for level in range(chip_bits + 1):
            total = total + weight(h, inner_bits + 1 + level) * dot_nt(lifted[h], hbuf[h, level])
        scaled = total * lax.rsqrt(jnp.mean(total * total, axis=-1, keepdims=True) + EPSILON)
        gated = (scaled * gates[h]).astype(BF16)
        for part in range(nz):
            mbuf[part, :, span[h]] = gated[part * rows : (part + 1) * rows]

    n_copies = [
        pltpu.make_async_remote_copy(
            mbuf.at[zpeer(d)], nbuf.at[z], ns_sem.at[d - 1], nr_sem.at[d - 1], **to(s, zpeer(d))
        )
        for d in range(1, nz)
    ]
    for copy in n_copies:
        copy.start()
    nbuf[z] = mbuf[z]

    def w_pass(d):
        place = wbuf.at[zfrom(d), :, my_half]
        return pltpu.make_async_remote_copy(
            place, place, ds_sem.at[d - 1], dr_sem.at[d - 1], **to(partner, z)
        )

    local_w.wait()
    for d in range(1, nz):
        w_copies[d - 1].wait_recv()
        w_pass(d).start()
    for d in range(1, nz):
        n_copies[d - 1].wait_recv()

    g_copies = [
        pltpu.make_async_remote_copy(
            nbuf, gbuf.at[d - 1], gs_sem.at[d - 1], gr_sem.at[d - 1], **to(qpeer(d), z)
        )
        for d in range(1, nq)
    ]
    for copy in g_copies:
        copy.start()
    for d in range(1, nz):
        w_pass(d).wait_recv()

    def project(source):
        total = None
        for group in range(nz):
            share = jnp.dot(source[group], wbuf[group], preferred_element_type=F32)
            share = share.astype(BF16).astype(F32)
            total = share if total is None else total + share
        return total.astype(BF16)

    out_copies = []
    for d in range(1, nq):
        g_copies[d - 1].wait_recv()
        ybuf[d - 1] = project(gbuf.at[d - 1])
        copy = pltpu.make_async_remote_copy(
            ybuf.at[d - 1], obuf.at[q], os_sem.at[d - 1], or_sem.at[nq - d - 1],
            **to(2 * qfrom(d) + c, z),
        )
        copy.start()
        out_copies.append(copy)
    obuf[q] = project(nbuf)
    for d in range(1, nq):
        pltpu.make_async_remote_copy(
            ybuf.at[d - 1], obuf.at[qfrom(d)], os_sem.at[d - 1], or_sem.at[d - 1], **to(qpeer(d), z)
        ).wait_recv()
    for chip in range(nq):
        o_ref[:, chip * width : (chip + 1) * width] = obuf[chip]

    for copy in w_copies + n_copies + g_copies + out_copies + [pair]:
        copy.wait_send()
    for d in range(1, nz):
        w_pass(d).wait_send()
    for d in range(1, nq):
        @pl.when(q + d < nq)
        def _():
            state_copy(d).wait_send()


def solution(mesh):
    ns, nz = mesh.shape["seq"], mesh.shape["head"]
    nq = ns // 2
    chip_bits = nq.bit_length() - 1

    def on_device(queries, keys, values, gate, log_forget, write_rate, level_weight, w_out):
        tok, feats = queries.shape
        heads = log_forget.shape[0]
        levels = level_weight.shape[1]
        model = w_out.shape[1]
        width = model // nq
        rows = tok // nz
        state = (heads, 2, DK, DK)
        dma = pltpu.SemaphoreType.DMA
        vmem = pl.BlockSpec(memory_space=pltpu.VMEM)
        return pl.pallas_call(
            functools.partial(kernel, ns, nz, heads, levels),
            out_shape=jax.ShapeDtypeStruct((rows, model), BF16),
            in_specs=[vmem] * 7 + [pl.BlockSpec(memory_space=pl.ANY)],
            out_specs=vmem,
            scratch_shapes=[
                pltpu.VMEM((128, tok), F32),
                pltpu.VMEM((nz, w_out.shape[0], width), BF16),
                pltpu.VMEM(state, BF16),
                pltpu.VMEM(state, BF16),
                pltpu.VMEM(state, BF16),
                pltpu.VMEM((nq - 1,) + state, BF16),
                pltpu.VMEM((heads, chip_bits + 1, DK, DK), F32),
                pltpu.VMEM((heads, DK, DK), F32),
                pltpu.VMEM((nz, rows, feats), BF16),
                pltpu.VMEM((nz, rows, feats), BF16),
                pltpu.VMEM((nq - 1, nz, rows, feats), BF16),
                pltpu.VMEM((nq - 1, rows, width), BF16),
                pltpu.VMEM((nq, rows, width), BF16),
                dma,
                dma((nz - 1,)),
                dma((nz - 1,)),
                dma((nz - 1,)),
                dma((nz - 1,)),
                dma,
                dma,
                dma((nq - 1,)),
                dma((nq - 1,)),
                dma((nz - 1,)),
                dma((nz - 1,)),
                dma((nq - 1,)),
                dma((nq - 1,)),
                dma((nq - 1,)),
                dma((nq - 1,)),
            ],
            compiler_params=pltpu.CompilerParams(collective_id=0, has_side_effects=True),
            name="fenwick_layer",
        )(queries, keys, values, gate, log_forget, write_rate, level_weight, w_out)

    in_specs = (
        P("seq", "head"),
        P("seq", "head"),
        P("seq", "head"),
        P("seq", "head"),
        P("head", "seq"),
        P("head", "seq"),
        P("head", None, "seq"),
        P("head", None),
    )
    out_specs = P(("seq", "head"), None)
    return jax.shard_map(
        on_device, mesh=mesh, in_specs=in_specs, out_specs=out_specs, check_vma=False
    )
```

time: 215 us -> 50.9 us (0.24)
  other arithmetic: 85.8 us -> 0 us
  waiting for transfers between devices: 49.4 us -> 0 us
  Pallas kernels: 0 us -> 47.5 us
  matrix products: 39.3 us -> 0 us
  local copies, waits for them, and re-layouts: 20.7 us -> 3.18 us
  between operations: 14 us -> 0.01 us
  starting transfers between devices: 5.23 us -> 0 us
    another operation x5 -> x0, other arithmetic: 79.6 us -> none  [the longest x1 40.2 us: on_device(): jax.scipy.linalg.solve_triangular(lower_keys, strength[..., None] * key_r...]
    pallas_call x0 -> x1, Pallas kernels: none -> 47.5 us  [on_device(): pl.pallas_call(functools.partial(kernel, ns, nz, heads, levels), out_shap...]
    reduce_scatter x1 -> x0, waiting for transfers between devices: 44.1 us -> none  [on_device(): lax.psum_scatter(jnp.dot(normed, w_out, preferred_element_type=jnp.float3...]
    dot_general x28 -> x0, matrix products: 36.2 us -> none  [the longest x15 14 us: matmul(): return jnp.einsum('...ij,...jk->...ik', left, right, precision=PRECISE)]
    slice x5 -> x0, local copies, waits for them, and re-layouts: 5.87 us -> none  [the longest x2 2.87 us: on_device(): weights[:, 1 + inner_bits:]]
    ppermute x5 -> x0, waiting for transfers between devices: 5.25 us -> none  [swapped(): return lax.ppermute(block, axis, route)]
    ppermute x5 -> x0, starting transfers between devices: 5.23 us -> none  [swapped(): return lax.ppermute(block, axis, route)]
    rev x4 -> x0, local copies, waits for them, and re-layouts: 3.92 us -> none  [partner_blocks(): return jnp.flip(shaped, axis=2).reshape(tensor.shape)]
  transfers between devices with their start and end apart: 6 -> 0, of which waited for: 3 -> 0; matrix products, arithmetic and copies ran while one was open for 16% -> 0% of each run, Pallas kernels for 0% -> 0%
where the time goes in v1:
time: 50.9 us; the launch traced here: 50.7 us
  Pallas kernels  47.5 us (93%)
  local copies, waits for them, and re-layouts  3.18 us (6%)
    pallas_call x1, Pallas kernels, on_device(): pl.pallas_call(functools.partial(kernel, ns, nz, heads, levels), out_shap...  47.5 us
    unnamed x2, local copies, waits for them, and re-layouts  3.18 us

profile of v1, /device:TPU:0, one launch (start us, length us, event | category | flops | bytes accessed | tf_op | source)
XLA Modules:
  0.0 50.7 jit_solution(9539346449524885105)
XLA Ops:
  0.0 1.3 %copy.9.lw_ref = f32[2,6,256]{2,1,0:T(8,128)} copy(f32[2,6,256]{2,0,1:T(2,128)} %param.14) | data formatting | bytes 24576 | tf_op args[6]
  1.3 47.5 %fenwick_layer.1 = bf16[64,4096]{1,0:T(8,128)(2,1)} custom-call(bf16[256,256]{1,0:T(8,128)(2,1)} %q_ref.1, bf16[256,256]{1,0:T(8,128)(2,1)} %k_ref.1, bf16[256,256]{1,0:T(8,128)(2,1)} %v_ref.1, bf16[256,256]{1,0:T(8,128)(2,1)} %g_ref.1, f32[2,256]{1,0:T(2,128)} %lf_ref.1, f32[2,256]{1,0:T(2,128)} %wr_ref.1, f32[2,6,256]{2,1,0:T(8,128)} %copy.9.lw_ref, ...), custom_call_target="tpu_custom_call" | custom-call | tf_op jit(solution)/shard_map/fenwick_layer/pallas_call | solution.py:298
  48.8 1.9 %copy.11 = bf16[64,4096]{1,0:T(8,128)(2,1)} copy(bf16[64,4096]{1,0:T(8,128)(2,1)} %fenwick_layer.1) | data formatting | bytes 1048576

commit v2 on v1

--- a/solution.py
+++ b/solution.py
@@ -33,8 +33,8 @@
 def kernel(
     ns, nz, heads, levels,
     q_ref, k_ref, v_ref, g_ref, lf_ref, wr_ref, lw_ref, w_ref, o_ref,
-    stage, wbuf, ebuf, pbuf, tbuf, sbuf, hbuf, pm, mbuf, nbuf, gbuf, ybuf, obuf,
-    wl_sem, ws_sem, wr_sem, ds_sem, dr_sem, ps_sem, pr_sem, ss_sem, sr_sem,
+    stage, wbuf, wrest, xbuf, rbuf, ebuf, pbuf, tbuf, sbuf, hbuf, pm, mbuf, nbuf, gbuf, ybuf, obuf,
+    wl_sem, wt_sem, xs_sem, xr_sem, ws_sem, wr_sem, ds_sem, dr_sem, ps_sem, pr_sem, ss_sem, sr_sem,
     ns_sem, nr_sem, gs_sem, gr_sem, os_sem, or_sem,
 ):
     tok = q_ref.shape[0]
@@ -77,6 +77,10 @@
     my_half = pl.ds(pl.multiple_of(c * half, half), half)
     local_w = pltpu.make_async_copy(w_ref.at[:, chip_cols], wbuf.at[z], wl_sem)
     local_w.start()
+    rest = w_ref.shape[1] - nq * width
+    if rest:
+        local_rest = pltpu.make_async_copy(w_ref.at[:, nq * width :], wrest, wt_sem)
+        local_rest.start()
     pl.semaphore_wait(barrier, nz + nq - 1)
 
     w_copies = [
@@ -220,6 +224,19 @@
         copy.start()
     nbuf[z] = mbuf[z]
 
+    x_copies = []
+    if rest:
+        local_rest.wait()
+        for d in range(1, nz):
+            share = jnp.dot(mbuf[zpeer(d)], wrest[...], preferred_element_type=F32)
+            xbuf[d - 1] = share.astype(BF16)
+            copy = pltpu.make_async_remote_copy(
+                xbuf.at[d - 1], rbuf.at[d - 1], xs_sem.at[d - 1], xr_sem.at[d - 1],
+                **to(s, zpeer(d)),
+            )
+            copy.start()
+            x_copies.append(copy)
+
     def w_pass(d):
         place = wbuf.at[zfrom(d), :, my_half]
         return pltpu.make_async_remote_copy(
@@ -252,6 +269,7 @@
             total = share if total is None else total + share
         return total.astype(BF16)
 
+    obuf[q] = project(nbuf)
     out_copies = []
     for d in range(1, nq):
         g_copies[d - 1].wait_recv()
@@ -262,7 +280,12 @@
         )
         copy.start()
         out_copies.append(copy)
-    obuf[q] = project(nbuf)
+    if rest:
+        total = jnp.dot(mbuf[z], wrest[...], preferred_element_type=F32).astype(BF16).astype(F32)
+        for d in range(1, nz):
+            x_copies[d - 1].wait_recv()
+            total = total + rbuf[d - 1].astype(F32)
+        o_ref[:, nq * width :] = total.astype(BF16)
     for d in range(1, nq):
         pltpu.make_async_remote_copy(
             ybuf.at[d - 1], obuf.at[qfrom(d)], os_sem.at[d - 1], or_sem.at[d - 1], **to(qpeer(d), z)
@@ -270,7 +293,7 @@
     for chip in range(nq):
         o_ref[:, chip * width : (chip + 1) * width] = obuf[chip]
 
-    for copy in w_copies + n_copies + g_copies + out_copies + [pair]:
+    for copy in w_copies + n_copies + x_copies + g_copies + out_copies + [pair]:
         copy.wait_send()
     for d in range(1, nz):
         w_pass(d).wait_send()
@@ -290,7 +313,9 @@
         heads = log_forget.shape[0]
         levels = level_weight.shape[1]
         model = w_out.shape[1]
-        width = model // nq
+        tiles = model // (DK * ns)
+        width = 2 * DK * (tiles - tiles // 4)
+        rest = max(model - nq * width, DK)
         rows = tok // nz
         state = (heads, 2, DK, DK)
         dma = pltpu.SemaphoreType.DMA
@@ -303,6 +328,9 @@
             scratch_shapes=[
                 pltpu.VMEM((128, tok), F32),
                 pltpu.VMEM((nz, w_out.shape[0], width), BF16),
+                pltpu.VMEM((w_out.shape[0], rest), BF16),
+                pltpu.VMEM((nz - 1, rows, rest), BF16),
+                pltpu.VMEM((nz - 1, rows, rest), BF16),
                 pltpu.VMEM(state, BF16),
                 pltpu.VMEM(state, BF16),
                 pltpu.VMEM(state, BF16),
@@ -315,6 +343,9 @@
                 pltpu.VMEM((nq - 1, rows, width), BF16),
                 pltpu.VMEM((nq, rows, width), BF16),
                 dma,
+                dma,
+                dma((nz - 1,)),
+                dma((nz - 1,)),
                 dma((nz - 1,)),
                 dma((nz - 1,)),
                 dma((nz - 1,)),

time: 50.9 us -> 49.9 us (0.980)
  Pallas kernels: 47.5 us -> 46.5 us
    pallas_call x1, Pallas kernels: 47.5 us -> 46.5 us  [on_device(): pl.pallas_call(functools.partial(kernel, ns, nz, heads, levels), out_shap...]
where the time goes in v2:
time: 49.9 us; the launch traced here: 49.7 us
  Pallas kernels  46.5 us (93%)
  local copies, waits for them, and re-layouts  3.18 us (6%)
    pallas_call x1, Pallas kernels, on_device(): pl.pallas_call(functools.partial(kernel, ns, nz, heads, levels), out_shap...  46.5 us
    unnamed x2, local copies, waits for them, and re-layouts  3.18 us

profile of v2, /device:TPU:0, one launch (start us, length us, event | category | flops | bytes accessed | tf_op | source)
XLA Modules:
  0.0 49.7 jit_solution(14087938127818463037)
XLA Ops:
  0.0 1.3 %copy.9.lw_ref = f32[2,6,256]{2,1,0:T(8,128)} copy(f32[2,6,256]{2,0,1:T(2,128)} %param.14) | data formatting | bytes 24576 | tf_op args[6]
  1.3 46.5 %fenwick_layer.1 = bf16[64,4096]{1,0:T(8,128)(2,1)} custom-call(bf16[256,256]{1,0:T(8,128)(2,1)} %q_ref.1, bf16[256,256]{1,0:T(8,128)(2,1)} %k_ref.1, bf16[256,256]{1,0:T(8,128)(2,1)} %v_ref.1, bf16[256,256]{1,0:T(8,128)(2,1)} %g_ref.1, f32[2,256]{1,0:T(2,128)} %lf_ref.1, f32[2,256]{1,0:T(2,128)} %wr_ref.1, f32[2,6,256]{2,1,0:T(8,128)} %copy.9.lw_ref, ...), custom_call_target="tpu_custom_call" | custom-call | tf_op jit(solution)/shard_map/fenwick_layer/pallas_call | solution.py:323
  47.8 1.9 %copy.11 = bf16[64,4096]{1,0:T(8,128)(2,1)} copy(bf16[64,4096]{1,0:T(8,128)(2,1)} %fenwick_layer.1) | data formatting | bytes 1048576

commit v3 on v2

--- a/solution.py
+++ b/solution.py
@@ -102,8 +102,8 @@
         stage[0:8, :], upto, precision=lax.Precision.HIGHEST, preferred_element_type=F32
     )
     stage[8 : 8 + heads, :] = wr_ref[...]
-    for h in range(heads):
-        stage[16 + h * levels : 16 + (h + 1) * levels, :] = lw_ref[h]
+    for level in range(levels):
+        stage[16 + level * heads : 16 + (level + 1) * heads, :] = lw_ref[level]
     cols = stage[...].T
     differ = lax.bitwise_xor(ti, ui)
     inclusive = ti >= ui
@@ -114,7 +114,7 @@
     b_col = [cols[:, 8 + h : 9 + h] for h in hs]
 
     def weight(h, level):
-        at = 16 + h * levels + level
+        at = 16 + level * heads + h
         return cols[:, at : at + 1]
 
     kn = [unit_rows(k_ref, span[h]) for h in hs]
@@ -222,6 +222,21 @@
     ]
     for copy in n_copies:
         copy.start()
+
+    order = sorted(range(1, nq), key=lambda d: abs(2 * d - nq))
+
+    def plane_copy(d, e):
+        group = zfrom(e)
+        return pltpu.make_async_remote_copy(
+            nbuf.at[group] if e else mbuf.at[z],
+            gbuf.at[d - 1, group],
+            gs_sem.at[d - 1, e],
+            gr_sem.at[d - 1, e],
+            **to(qpeer(d), z),
+        )
+
+    for d in order:
+        plane_copy(d, 0).start()
     nbuf[z] = mbuf[z]
 
     x_copies = []
@@ -243,21 +258,14 @@
             place, place, ds_sem.at[d - 1], dr_sem.at[d - 1], **to(partner, z)
         )
 
+    for e in range(1, nz):
+        n_copies[e - 1].wait_recv()
+        for d in order:
+            plane_copy(d, e).start()
     local_w.wait()
     for d in range(1, nz):
         w_copies[d - 1].wait_recv()
         w_pass(d).start()
-    for d in range(1, nz):
-        n_copies[d - 1].wait_recv()
-
-    g_copies = [
-        pltpu.make_async_remote_copy(
-            nbuf, gbuf.at[d - 1], gs_sem.at[d - 1], gr_sem.at[d - 1], **to(qpeer(d), z)
-        )
-        for d in range(1, nq)
-    ]
-    for copy in g_copies:
-        copy.start()
     for d in range(1, nz):
         w_pass(d).wait_recv()
 
@@ -271,8 +279,9 @@
 
     obuf[q] = project(nbuf)
     out_copies = []
-    for d in range(1, nq):
-        g_copies[d - 1].wait_recv()
+    for d in order:
+        for e in range(nz):
+            plane_copy(d, e).wait_recv()
         ybuf[d - 1] = project(gbuf.at[d - 1])
         copy = pltpu.make_async_remote_copy(
             ybuf.at[d - 1], obuf.at[q], os_sem.at[d - 1], or_sem.at[nq - d - 1],
@@ -293,10 +302,13 @@
     for chip in range(nq):
         o_ref[:, chip * width : (chip + 1) * width] = obuf[chip]
 
-    for copy in w_copies + n_copies + x_copies + g_copies + out_copies + [pair]:
+    for copy in w_copies + n_copies + x_copies + out_copies + [pair]:
         copy.wait_send()
     for d in range(1, nz):
         w_pass(d).wait_send()
+    for d in range(1, nq):
+        for e in range(nz):
+            plane_copy(d, e).wait_send()
     for d in range(1, nq):
         @pl.when(q + d < nq)
         def _():
@@ -356,14 +368,14 @@
                 dma((nq - 1,)),
                 dma((nz - 1,)),
                 dma((nz - 1,)),
-                dma((nq - 1,)),
-                dma((nq - 1,)),
+                dma((nq - 1, nz)),
+                dma((nq - 1, nz)),
                 dma((nq - 1,)),
                 dma((nq - 1,)),
             ],
             compiler_params=pltpu.CompilerParams(collective_id=0, has_side_effects=True),
             name="fenwick_layer",
-        )(queries, keys, values, gate, log_forget, write_rate, level_weight, w_out)
+        )(queries, keys, values, gate, log_forget, write_rate, jnp.swapaxes(level_weight, 0, 1), w_out)
 
     in_specs = (
         P("seq", "head"),

time: 49.9 us -> 46.8 us (0.938)
  Pallas kernels: 46.5 us -> 44.8 us
  local copies, waits for them, and re-layouts: 3.18 us -> 1.87 us
    pallas_call x1, Pallas kernels: 46.5 us -> 44.8 us  [on_device(): pl.pallas_call(functools.partial(kernel, ns, nz, heads, levels), out_shap...]
    unnamed x2 -> x1, local copies, waits for them, and re-layouts: 3.18 us -> 1.87 us
where the time goes in v3:
time: 46.8 us; the launch traced here: 46.7 us
  Pallas kernels  44.8 us (96%)
  local copies, waits for them, and re-layouts  1.87 us (4%)
    pallas_call x1, Pallas kernels, on_device(): pl.pallas_call(functools.partial(kernel, ns, nz, heads, levels), out_shap...  44.8 us
    unnamed x1, local copies, waits for them, and re-layouts  1.87 us

profile of v3, /device:TPU:0, one launch (start us, length us, event | category | flops | bytes accessed | tf_op | source)
XLA Modules:
  0.0 46.7 jit_solution(16895078064751458524)
XLA Ops:
  0.0 44.8 %fenwick_layer.1 = bf16[64,4096]{1,0:T(8,128)(2,1)} custom-call(bf16[256,256]{1,0:T(8,128)(2,1)} %q_ref.1, bf16[256,256]{1,0:T(8,128)(2,1)} %k_ref.1, bf16[256,256]{1,0:T(8,128)(2,1)} %v_ref.1, bf16[256,256]{1,0:T(8,128)(2,1)} %g_ref.1, f32[2,256]{1,0:T(2,128)} %lf_ref.1, f32[2,256]{1,0:T(2,128)} %wr_ref.1, f32[6,2,256]{2,1,0:T(2,128)} %bitcast.1, ...), custom_call_target="tpu_custom_call" | custom-call | tf_op jit(solution)/shard_map/fenwick_layer/pallas_call | solution.py:335
  44.8 1.9 %copy.10 = bf16[64,4096]{1,0:T(8,128)(2,1)} copy(bf16[64,4096]{1,0:T(8,128)(2,1)} %fenwick_layer.1) | data formatting | bytes 1048576
